TPU v7x, 32 devices: a 4x2x2 block of a 4x4x8 slice. The times are simulated.
32 devices in a mesh: dp: 4 (over y, z), tp: 8 (over x, core).
Axes of the slice: x: 4, y: 2, z: 2, core: 2. Of those that a mesh axis runs over, the one named last changes fastest.
The devices are a block of a 4x4x8 slice.
Arguments:
- x: bfloat16 [8, 2048, 4096], P('dp'), parts along dimension 0
- gamma: float32 [4096], replicated
- beta: float32 [4096], replicated
- wqkv: bfloat16 [4096, 12288], P(None, 'tp')
- wo: bfloat16 [16, 256, 4096], P('tp')
- w1: bfloat16 [4096, 16384], P(None, 'tp')
- w2: bfloat16 [16384, 4096], P('tp')
Outputs:
- output: bfloat16 [8, 2048, 4096], P('dp'), parts along dimension 0
There are 4 independent parts. A program takes and returns all parts, laid end to end along the dimension named above; an argument that names none is the same for every part.
All inputs are finite; a program needn't handle non-finite values.
Results may differ from a plain program's by a relative error of at most 0.0104537.
Values are sent between devices in bfloat16 or wider.
A program may use at most 768 MiB of HBM per device.

v0:
```python
import functools
import jax
import jax.numpy as jnp
from jax import lax
from jax.sharding import PartitionSpec as P


def layer_norm(x, gamma, beta):
    xf = x.astype(jnp.float32)
    mu = jnp.mean(xf, axis=-1, keepdims=True)
    var = jnp.mean(jnp.square(xf - mu), axis=-1, keepdims=True)
    return ((xf - mu) * lax.rsqrt(var + 1e-5) * gamma + beta).astype(jnp.bfloat16)


def attend(qkv_b, hpg):
    s = qkv_b.shape[0]
    dh = qkv_b.shape[-1]
    q = qkv_b[:, :, :hpg]
    k = qkv_b[:, :, hpg]
    v = qkv_b[:, :, hpg + 1]
    sc = jnp.einsum('sghd,tgd->ghst', q, k, preferred_element_type=jnp.float32) * (dh ** -0.5)
    pos = jnp.arange(s)
    sc = jnp.where((pos[:, None] >= pos[None, :])[None, None], sc, -1e30)
    p = jax.nn.softmax(sc, axis=-1).astype(jnp.bfloat16)
    o = jnp.einsum('ghst,tgd->sghd', p, v, preferred_element_type=jnp.float32)
    return o.astype(jnp.bfloat16).reshape(s, -1)


def solution(mesh):
    def local(x, gamma, beta, wqkv, wo, w1, w2):
        b, s, d = x.shape
        hl, dh, _ = wo.shape
        gl = (wqkv.shape[1] - hl * dh) // (2 * dh)
        hpg = hl // gl
        ntok = b * s
        ln = layer_norm(x, gamma, beta).reshape(ntok, d)
        qkv = jnp.dot(ln, wqkv, preferred_element_type=jnp.float32).astype(jnp.bfloat16)
        o = lax.map(functools.partial(attend, hpg=hpg), qkv.reshape(b, s, gl, hpg + 2, dh))
        a = jnp.dot(o.reshape(ntok, hl * dh), wo.reshape(hl * dh, d), preferred_element_type=jnp.float32)
        hmid = jax.nn.gelu(jnp.dot(ln, w1, preferred_element_type=jnp.float32), approximate=False).astype(jnp.bfloat16)
        part_sum = (a + jnp.dot(hmid, w2, preferred_element_type=jnp.float32)).astype(jnp.bfloat16)
        total = lax.psum(part_sum, 'tp')
        return (x.astype(jnp.float32) + total.astype(jnp.float32).reshape(b, s, d)).astype(jnp.bfloat16)

    return jax.shard_map(local, mesh=mesh,
                         in_specs=(P('dp', None, None), P(None), P(None), P(None, 'tp'),
                                   P('tp', None, None), P(None, 'tp'), P('tp', None)),
                         out_specs=P('dp', None, None), check_vma=False)
```

profile of v0, /device:TPU:81, one launch (start us, length us, event | category | flops | bytes accessed | tf_op | source)
XLA Modules:
  0.0 939.4 jit_solution(9764900615591596358)
XLA Ops:
  6.6 11.2 %convert_reduce_fusion = f32[2,2048]{1,0:T(2,128)S(1)} fusion(bf16[2,2048,4096]{2,1,0:T(8,128)(2,1)} %param.9), kind=kLoop, calls=%fused_computation.19 | loop fusion | flops 33550336 | bytes 33570816 | tf_op jit(solution)/shard_map/reduce_sum | solution.py:10
  17.8 12.9 %fusion.12 = f32[2,2048]{1,0:T(2,128)S(1)} fusion(bf16[2,2048,4096]{2,1,0:T(8,128)(2,1)} %param.9, f32[2,2048]{1,0:T(2,128)S(1)} %broadcast_multiply_fusion), kind=kLoop, calls=%fused_computation.22 | loop fusion | flops 67104768 | bytes 33587200 | tf_op jit(solution)/shard_map/reduce_sum | solution.py:11
  30.7 23.4 %fusion.15 = bf16[2,2048,4096]{2,1,0:T(8,128)(2,1)} fusion(bf16[2,2048,4096]{2,1,0:T(8,128)(2,1)} %param.9, f32[4096]{0:T(1024)S(1)} %copy-done.1, f32[4096]{0:T(1024)S(1)} %copy-done.2, f32[2,2048]{1,0:T(2,128)S(1)} %add_rsqrt_fusion, f32[2,2048]{1,0:T(2,128)S(1)} %broadcast_multiply_fusion), kind=kLoop, calls=%fused_computation.25 | loop fusion | flops 100663296 | bytes 67174400 | tf_op jit(solution)/shard_map/convert_element_type | solution.py:12
  54.1 60.2 %convolution_convert_fusion = bf16[4096,1536]{1,0:T(8,128)(2,1)} fusion(bf16[4096,4096]{1,0:T(8,128)(2,1)} %bitcast.73, bf16[4096,1536]{1,0:T(8,128)(2,1)} %param.12), kind=kOutput, calls=%fused_computation.77 | convolution fusion | flops 51545899008 | bytes 58720256 | tf_op jit(solution)/shard_map/dot_general | solution.py:37
  114.3 78.3 %fusion.89 = f32[4096,2048]{1,0:T(8,128)} fusion(bf16[4096,4096]{1,0:T(8,128)(2,1)} %bitcast.74, bf16[4096,2048]{1,0:T(8,128)(2,1)} %param.14), kind=kOutput, calls=%fused_computation.111 | convolution fusion | flops 68719476736 | bytes 83886080 | tf_op jit(solution)/shard_map/dot_general | solution.py:40
  192.6 47.7 %reshape.75 = bf16[2,2048,2,3,256]{4,3,2,1,0:T(4,128)(2,1)} reshape(bf16[4096,1536]{1,0:T(8,128)(2,1)} %convolution_convert_fusion) | data formatting | bytes 25165824 | tf_op jit(solution)/shard_map/reshape | solution.py:38
  240.3 13.4 %copy.14 = bf16[2,2048,2,3,256]{4,1,2,3,0:T(8,128)(2,1)} copy(bf16[2,2048,2,3,256]{4,3,2,1,0:T(4,128)(2,1)} %reshape.75) | data formatting | bytes 25165824 | tf_op jit(solution)/shard_map/while | solution.py:38
  253.7 131.9 %while.10 = (s32[]{:T(128)}, bf16[2,2048,512]{2,1,0:T(8,128)(2,1)}, bf16[2,2048,2,3,256]{4,1,2,3,0:T(8,128)(2,1)}, s32[]{:T(128)}) while((s32[]{:T(128)}, bf16[2,2048,512]{2,1,0:T(8,128)(2,1)}, bf16[2,2048,2,3,256]{4,1,2,3,0:T(8,128)(2,1)}, s32[]{:T(128)}) %tuple.23), condition=%wide.region_5.6_spmd, body=%wide.region_2.5_spmd.sunk | while | flops 8695832576 | bytes 182534288 | solution.py:38
  253.7 4.2 iota_compare_fusion.2
  257.9 5.8 dynamic-slice_bitcast_fusion.2
  263.7 17.7 %fusion.105 = (f32[2,2048]{1,0:T(2,128)S(1)}, f32[2,2048,2048]{2,1,0:T(8,128)}) fusion(pred[2048,2048]{0,1:T(8,128)(4,1)} %iota_compare_fusion.2, bf16[2048,2,3,256]{3,0,1,2:T(8,128)(2,1)} %dynamic-slice_bitcast_fusion.2), kind=kOutput, calls=%fused_computation.4.clone.1 | convolution fusion | flops 4320129024 | bytes 41959424 | tf_op jit(solution)/shard_map/while/body/eval_jaxpr/sghd,tgd->ghst/dot_general | solution.py:21
  281.4 0.0 slice-start
  281.4 0.0 slice-start.1
  281.4 16.8 %fusion.106 = f32[2,2048]{1,0:T(2,128)S(1)} fusion(f32[2,2048,2048]{2,1,0:T(8,128)} %get-tuple-element.58, f32[2,2048]{1,0:T(2,128)S(1)} %get-tuple-element.59, pred[2048,2048]{0,1:T(8,128)(4,1)} %iota_compare_fusion.2), kind=kLoop, calls=%fused_computation.3.clone.1 | loop fusion | flops 33550336 | bytes 37781504 | tf_op jit(solution)/shard_map/while/body/eval_jaxpr/reduce_sum | solution.py:24
  298.2 17.2 %fusion.107 = bf16[2,256,2048]{2,1,0:T(8,128)(2,1)} fusion(f32[2,2048]{1,0:T(2,128)S(1)} %fusion.106, f32[2,2048]{1,0:T(2,128)S(1)} %get-tuple-element.59, f32[2,2048,2048]{2,1,0:T(8,128)} %get-tuple-element.58, pred[2048,2048]{0,1:T(8,128)(4,1)S(1)} %copy-done, bf16[2048,2,3,256]{3,0,1,2:T(8,128)(2,1)S(1)} %bitcast.71), kind=kOutput, calls=%fused_computation.9.clone.1 | convolution fusion | flops 4337958912 | bytes 41975808 | tf_op jit(solution)/shard_map/while/body/eval_jaxpr/ghst,tgd->sghd/dot_general | solution.py:25
  315.4 2.9 copy.23
  318.3 1.4 constant_dynamic-update-slice_fusion.2
  319.7 4.2 iota_compare_fusion.2
  323.9 5.8 dynamic-slice_bitcast_fusion.2
  329.7 17.7 %fusion.105 = (f32[2,2048]{1,0:T(2,128)S(1)}, f32[2,2048,2048]{2,1,0:T(8,128)}) fusion(pred[2048,2048]{0,1:T(8,128)(4,1)} %iota_compare_fusion.2, bf16[2048,2,3,256]{3,0,1,2:T(8,128)(2,1)} %dynamic-slice_bitcast_fusion.2), kind=kOutput, calls=%fused_computation.4.clone.1 | convolution fusion | flops 4320129024 | bytes 41959424 | tf_op jit(solution)/shard_map/while/body/eval_jaxpr/sghd,tgd->ghst/dot_general | solution.py:21
  347.4 0.0 slice-start
  347.4 0.0 slice-start.1
  347.4 16.8 %fusion.106 = f32[2,2048]{1,0:T(2,128)S(1)} fusion(f32[2,2048,2048]{2,1,0:T(8,128)} %get-tuple-element.58, f32[2,2048]{1,0:T(2,128)S(1)} %get-tuple-element.59, pred[2048,2048]{0,1:T(8,128)(4,1)} %iota_compare_fusion.2), kind=kLoop, calls=%fused_computation.3.clone.1 | loop fusion | flops 33550336 | bytes 37781504 | tf_op jit(solution)/shard_map/while/body/eval_jaxpr/reduce_sum | solution.py:24
  364.2 0.0 copy-done
  364.2 17.2 %fusion.107 = bf16[2,256,2048]{2,1,0:T(8,128)(2,1)} fusion(f32[2,2048]{1,0:T(2,128)S(1)} %fusion.106, f32[2,2048]{1,0:T(2,128)S(1)} %get-tuple-element.59, f32[2,2048,2048]{2,1,0:T(8,128)} %get-tuple-element.58, pred[2048,2048]{0,1:T(8,128)(4,1)S(1)} %copy-done, bf16[2048,2,3,256]{3,0,1,2:T(8,128)(2,1)S(1)} %bitcast.71), kind=kOutput, calls=%fused_computation.9.clone.1 | convolution fusion | flops 4337958912 | bytes 41975808 | tf_op jit(solution)/shard_map/while/body/eval_jaxpr/ghst,tgd->sghd/dot_general | solution.py:25
  381.4 2.9 copy.23
  384.2 1.4 constant_dynamic-update-slice_fusion.2
  385.7 30.0 %fusion.88 = f32[4096,4096]{1,0:T(8,128)} fusion(bf16[4096,512]{1,0:T(8,128)(2,1)} %bitcast.77, bf16[512,4096]{1,0:T(8,128)(2,1)} %bitcast.76), kind=kOutput, calls=%fused_computation.110 | convolution fusion | flops 17179869184 | bytes 75497472 | tf_op jit(solution)/shard_map/dot_general | solution.py:39
  415.6 145.4 %add_convert_fusion = bf16[4096,4096]{1,0:T(8,128)(2,1)} fusion(f32[4096,4096]{1,0:T(8,128)} %fusion.88, bf16[2048,4096]{1,0:T(8,128)(2,1)} %param.15, f32[4096,2048]{1,0:T(8,128)} %fusion.89), kind=kOutput, calls=%fused_computation.27 | convolution fusion | flops 69298290688 | bytes 150994944 | tf_op jit(solution)/shard_map/dot_general | solution.py:41
  561.1 0.1 all-reduce.2.cloned.1.call-update
  561.1 337.9 %all-reduce.2.cloned.1.call-done = bf16[2,2048,4096]{2,1,0:T(8,128)(2,1)} async-done(((bf16[2,2048,4096]{2,1,0:T(8,128)(2,1)}), bf16[2,2048,4096]{2,1,0:T(8,128)(2,1)}) %all-reduce.2.cloned.1.call-update) | async-done | bytes 33554448 | tf_op jit(solution)/shard_map/psum | solution.py:42
  899.0 33.1 %fusion.16 = bf16[2,2048,4096]{2,1,0:T(8,128)(2,1)} fusion(bf16[2,2048,4096]{2,1,0:T(8,128)(2,1)} %param.9, bf16[2,2048,4096]{2,1,0:T(8,128)(2,1)} %all-reduce.2.cloned.1.call-done), kind=kLoop, calls=%fused_computation.26 | loop fusion | flops 67108864 | bytes 100663296 | tf_op jit(solution)/shard_map/convert_element_type | solution.py:43
  (17 shorter events, 0.1 us)
Async XLA Ops:
  6.5 892.5 %all-reduce.2.cloned.1.call-start = ((), (), s32[]{:S(2)}) async-start(), calls=%async_computation | async-start | bytes 67108864 | tf_op jit(solution)/shard_map/psum | solution.py:42
  6.6 24.2 %copy-start.1 = (f32[4096]{0:T(1024)S(1)}, f32[4096]{0:T(1024)}, u32[]{:S(2)}) copy-start(f32[4096]{0:T(1024)} %param.11) | copy-start | bytes 49156
  6.6 24.2 %copy-start.2 = (f32[4096]{0:T(1024)S(1)}, f32[4096]{0:T(1024)}, u32[]{:S(2)}) copy-start(f32[4096]{0:T(1024)} %param.10) | copy-start | bytes 49156
  281.4 16.8 %copy-start = (pred[2048,2048]{0,1:T(8,128)(4,1)S(1)}, pred[2048,2048]{0,1:T(8,128)(4,1)}, u32[]{:S(2)}) copy-start(pred[2048,2048]{0,1:T(8,128)(4,1)} %iota_compare_fusion.2) | copy-start | bytes 12582916 | tf_op jit(solution)/shard_map/while
  281.4 16.8 %slice-start = ((s8[6291456]{0:T(1024)(128)(4,1)}), s8[4194304]{0:T(1024)(128)(4,1)S(1)}, s32[]{:S(2)}) async-start(s8[6291456]{0:T(1024)(128)(4,1)} %bitcast.70), calls=%async_computation.1 | async-start | bytes 8388608 | tf_op jit(solution)/shard_map/while
  281.4 16.8 %slice-start.1 = ((s8[6291456]{0:T(1024)(128)(4,1)}), s8[2097152]{0:T(1024)(128)(4,1)S(1)}, s32[]{:S(2)}) async-start(s8[6291456]{0:T(1024)(128)(4,1)} %bitcast.70), calls=%async_computation.2 | async-start | bytes 4194304 | tf_op jit(solution)/shard_map/while
  347.4 16.8 %copy-start = (pred[2048,2048]{0,1:T(8,128)(4,1)S(1)}, pred[2048,2048]{0,1:T(8,128)(4,1)}, u32[]{:S(2)}) copy-start(pred[2048,2048]{0,1:T(8,128)(4,1)} %iota_compare_fusion.2) | copy-start | bytes 12582916 | tf_op jit(solution)/shard_map/while
  347.4 16.8 %slice-start = ((s8[6291456]{0:T(1024)(128)(4,1)}), s8[4194304]{0:T(1024)(128)(4,1)S(1)}, s32[]{:S(2)}) async-start(s8[6291456]{0:T(1024)(128)(4,1)} %bitcast.70), calls=%async_computation.1 | async-start | bytes 8388608 | tf_op jit(solution)/shard_map/while
  347.4 16.8 %slice-start.1 = ((s8[6291456]{0:T(1024)(128)(4,1)}), s8[2097152]{0:T(1024)(128)(4,1)S(1)}, s32[]{:S(2)}) async-start(s8[6291456]{0:T(1024)(128)(4,1)} %bitcast.70), calls=%async_computation.2 | async-start | bytes 4194304 | tf_op jit(solution)/shard_map/while
Sparse Core Ops, SparseCore 0:
  561.3 337.7 all-reduce.1
where the time goes:
time: 948 us; the launch traced here: 939 us
  matrix products  384 us (41%)
  waiting for transfers between devices  338 us (36%)
  other arithmetic  122 us (13%)
  local copies, waits for them, and re-layouts  81.4 us (9%)
  between operations  13.9 us (1%)
    psum x1, waiting for transfers between devices, local(): total = lax.psum(part_sum, 'tp')  338 us
    dot_general x1, matrix products, local(): jnp.dot(hmid, w2, preferred_element_type=jnp.float32)  145 us
    dot_general x1, matrix products, local(): jnp.dot(ln, w1, preferred_element_type=jnp.float32)  78.3 us
    dot_general x1, matrix products, local(): jnp.dot(ln, wqkv, preferred_element_type=jnp.float32).astype(jnp.bfloat16)  60.2 us
    reshape x1, local copies, waits for them, and re-layouts, local(): qkv.reshape(b, s, gl, hpg + 2, dh)  47.7 us
    dot_general x2, matrix products, attend(): jnp.einsum('sghd,tgd->ghst', q, k, preferred_element_type=jnp.float32)  35.4 us
    dot_general x2, matrix products, attend(): o = jnp.einsum('ghst,tgd->sghd', p, v, preferred_element_type=jnp.float32)  34.3 us
    reduce_sum x2, other arithmetic, attend(): p = jax.nn.softmax(sc, axis=-1).astype(jnp.bfloat16)  33.5 us
  transfers between devices with their start and end apart: 1, of which 1 were waited for; matrix products, arithmetic and copies ran while one was open for 0% of the time, Pallas kernels for 0%

commit v1 on v0

v1 whole, which is shorter than its diff:
```python
import functools

import jax
import jax.numpy as jnp
from jax import lax
from jax.experimental import pallas as pl
from jax.experimental.pallas import tpu as pltpu
from jax.sharding import PartitionSpec as P

MESH = pl.DeviceIdType.MESH
F32 = jnp.float32
BF16 = jnp.bfloat16
BT = 512
NT = 512
NSLOT = 3
LOG2E = 1.4426950408889634


def dot(a, b):
    return jnp.dot(a, b, preferred_element_type=F32)


def gelu(x):
    return 0.5 * x * (1.0 + lax.erf(x * 0.7071067811865476))


def kernel(tp, seq, heads, dh,
           x, gamma, beta, wqkv, wo, w1, w2, y,
           wbuf, xbuf, ln, qkv, sc, h, pt, pr, cs, own, rs, relay, yt, xt, mx, acc,
           wsem, wosem, xsem, xtsem, ysem, psend, precv, ssem, rsem):
    t = lax.axis_index('tp')
    nx = tp // 2
    d, c = t // 2, t % 2
    left = lax.rem(d + nx - 1, nx)
    right = lax.rem(d + 1, nx)
    opp = lax.rem(d + 2, nx)
    partner = {'tp': d * 2 + (1 - c)}
    dev_l = {'tp': left * 2 + c}
    dev_r = {'tp': right * 2 + c}

    ntok, dm = x.shape
    nb = ntok // BT
    jb = seq // BT
    hw = heads * dh
    ff = w1.shape[1]
    nq = wqkv.shape[1] // NT
    nf = ff // NT
    hb = BT // 2
    LR = BT // (2 * nx)
    sub = NT // 2

    def tile(cc, o):
        return pl.multiple_of((cc * nx + o) * NT, NT)

    def ds_rows(b, off=0, n=BT):
        return pl.ds(pl.multiple_of(b * BT + off, hb), n)

    def w_q(i, slot):
        return [pltpu.make_async_copy(wqkv.at[:, pl.ds(pl.multiple_of(i * NT, NT), NT)], wbuf.at[slot], wsem.at[slot])]

    def w_f(i, slot):
        return [pltpu.make_async_copy(w1.at[:, pl.ds(pl.multiple_of(i * NT, NT), NT)], wbuf.at[slot], wsem.at[slot])]

    def owner(k):
        if isinstance(k, int):
            return (opp, right, left, d)[k]
        return lax.rem(d + jnp.where(k == 2, nx - 1, jnp.where(k == 3, 0, 2 - k)), nx)

    def w_o(cc, k, slot):
        col = tile(cc, owner(k))
        return [pltpu.make_async_copy(w2.at[:, pl.ds(col, NT)], wbuf.at[slot, pl.ds(0, ff)], wsem.at[slot]),
                pltpu.make_async_copy(wo.at[:, pl.ds(col, NT)], wbuf.at[slot, pl.ds(ff, hw)], wosem.at[slot])]

    def start(copies):
        for cp in copies:
            cp.start()

    def wait(copies):
        for cp in copies:
            cp.wait()

    def rc(i, src, dst, dev):
        return pltpu.make_async_remote_copy(src_ref=src, dst_ref=dst, send_sem=ssem.at[i], recv_sem=rsem.at[i],
                                            device_id=dev, device_id_type=MESH)

    rows_a, rows_b = pl.ds(0, hb), pl.ds(hb, hb)
    rs_opp_r = rc(0, cs.at[0, rows_b], relay.at[0], dev_r)
    rs_opp_l = rc(1, cs.at[0, rows_a], relay.at[1], dev_l)
    rs_dir_r = rc(2, cs.at[1, rows_a], rs.at[0], dev_r)
    rs_dir_l = rc(3, cs.at[2, rows_b], rs.at[1], dev_l)
    rs_cmb_r = rc(4, cs.at[1, rows_b], rs.at[2], dev_r)
    rs_cmb_l = rc(5, cs.at[2, rows_a], rs.at[3], dev_l)

    def ag_own(b):
        dst = y.at[ds_rows(b), pl.ds(tile(c, d), NT)]
        return rc(6, yt, dst, dev_r), rc(7, yt, dst, dev_l), rc(8, yt, dst, partner)

    def ag_own_arrived(b):
        def at(i, cc, o, dev):
            ref = y.at[ds_rows(b), pl.ds(tile(cc, o), NT)]
            return rc(i, yt, ref, dev)
        return at(6, c, left, dev_r), at(7, c, right, dev_l), at(8, 1 - c, d, partner)

    def y_tile(b, cc, o, off, n):
        return y.at[ds_rows(b, off, n), pl.ds(tile(cc, o), NT)]

    def ag_fwd(b):
        fb = y_tile(b, c, left, hb, hb)
        fa = y_tile(b, c, right, 0, hb)
        tl = y_tile(b, c, left, 0, BT)
        tr = y_tile(b, c, right, 0, BT)
        return (rc(9, fb, fb, dev_r), rc(10, fa, fa, dev_l), rc(11, tl, tl, partner), rc(12, tr, tr, partner))

    def ag_fwd_arrived(b):
        fb = y_tile(b, c, opp, hb, hb)
        fa = y_tile(b, c, opp, 0, hb)
        tl = y_tile(b, 1 - c, left, 0, BT)
        tr = y_tile(b, 1 - c, right, 0, BT)
        return (rc(9, fb, fb, dev_r), rc(10, fa, fa, dev_l), rc(11, tl, tl, partner), rc(12, tr, tr, partner))

    def ag_opp(b, cc):
        ref = y_tile(b, cc, opp, 0, BT)
        return rc(13, ref, ref, partner)

    def ptile(k):
        return pltpu.make_async_remote_copy(src_ref=pt.at[k], dst_ref=pr.at[k], send_sem=psend.at[k],
                                            recv_sem=precv.at[k], device_id=partner, device_id_type=MESH)

    def xt_copy(b):
        return pltpu.make_async_copy(x.at[ds_rows(b), pl.ds(tile(c, d), NT)], xt, xtsem)

    def yt_copy(b):
        return pltpu.make_async_copy(yt, y.at[ds_rows(b), pl.ds(tile(c, d), NT)], ysem)

    def x_copy(b):
        return pltpu.make_async_copy(x.at[ds_rows(b)], xbuf, xsem)

    def layer_norm(r0, n):
        for i in range(n // 16):
            r = pl.ds(pl.multiple_of(r0 + i * 16, 16), 16)
            v = xbuf[r, :].astype(F32)
            mu = jnp.sum(v, axis=-1, keepdims=True) * (1.0 / dm)
            v = v - mu
            var = jnp.sum(v * v, axis=-1, keepdims=True) * (1.0 / dm)
            ln[r, :] = (v * lax.rsqrt(var + 1e-5) * gamma[...] + beta[...]).astype(BF16)

    def t1():
        rs_opp_r.wait_recv()
        rs_opp_l.wait_recv()
        cs[1, hb:, :] = (cs[1, hb:, :].astype(F32) + relay[0].astype(F32)).astype(BF16)
        cs[2, :hb, :] = (cs[2, :hb, :].astype(F32) + relay[1].astype(F32)).astype(BF16)

    def t1_send():
        rs_cmb_r.start()
        rs_cmb_l.start()

    def t2(b):
        rs_dir_r.wait_recv()
        rs_dir_l.wait_recv()
        rs_cmb_r.wait_recv()
        rs_cmb_l.wait_recv()
        xt_copy(b).wait()

        def rows(r, p, q):
            tot = own[r, :] + (rs[p].astype(F32) + rs[q].astype(F32))
            yt[r, :] = (xt[r, :].astype(F32) + tot.astype(BF16).astype(F32)).astype(BF16)
        rows(slice(0, hb), 0, 3)
        rows(slice(hb, BT), 1, 2)

    def t3(b):
        for cp in ag_own(b):
            cp.start()
        yt_copy(b).start()

    def t4(b):
        al, ar, _ = ag_own_arrived(b)
        al.wait_recv()
        ar.wait_recv()
        for cp in ag_fwd(b):
            cp.start()
        for cp in (rs_opp_r, rs_opp_l, rs_dir_r, rs_dir_l, rs_cmb_r, rs_cmb_l):
            cp.wait_send()

    def t4_partner(b):
        ag_own_arrived(b)[2].wait_recv()
        for k in range(nx):
            ptile(k).wait_send()

    def t5(b):
        fb, fa, _, _ = ag_fwd_arrived(b)
        fb.wait_recv()
        fa.wait_recv()
        ag_opp(b, c).start()
        for cp in ag_own(b):
            cp.wait_send()
        yt_copy(b).wait()

    def t6(b):
        _, _, tl, tr = ag_fwd_arrived(b)
        tl.wait_recv()
        tr.wait_recv()
        ag_opp(b, 1 - c).wait_recv()
        for cp in ag_fwd(b):
            cp.wait_send()
        ag_opp(b, c).wait_send()

    start(w_q(0, 0))
    start(w_q(1, 1))
    x_copy(0).start()
    bar = pltpu.get_barrier_semaphore()
    for dev in (dev_l, dev_r, partner):
        pl.semaphore_signal(bar, inc=1, device_id=dev, device_id_type=MESH)
    x_copy(0).wait()

    @pl.loop(0, 2 * nx)
    def _(i):
        layer_norm(i * LR, LR)

    pl.semaphore_wait(bar, 3)

    def attention(j):
        scale = (dh ** -0.5) * LOG2E
        qr = pl.ds(pl.multiple_of(j * BT, BT), BT)
        for g in range(heads):
            q0, k0, v0 = g * 3 * dh, g * 3 * dh + dh, g * 3 * dh + 2 * dh
            q = qkv[qr, q0:q0 + dh]

            def lanes(s):
                m = s[:, :128]
                for n in range(1, BT // 128):
                    m = jnp.maximum(m, s[:, n * 128:(n + 1) * 128])
                return m

            def scores(kc):
                kr = pl.ds(pl.multiple_of(kc * BT, BT), BT)
                return lax.dot_general(q, qkv[kr, k0:k0 + dh], (((1,), (1,)), ((), ())), preferred_element_type=F32)

            s = scores(j)
            keep = lax.broadcasted_iota(jnp.int32, (BT, BT), 0) >= lax.broadcasted_iota(jnp.int32, (BT, BT), 1)
            s = jnp.where(keep, s, -1e30)
            sc[j] = s
            mx[...] = lanes(s)

            @pl.loop(0, j)
            def _(kc):
                s = scores(kc)
                sc[kc] = s
                mx[...] = jnp.maximum(mx[...], lanes(s))

            m = jnp.max(mx[...], axis=1, keepdims=True)
            mx[...] = jnp.zeros_like(mx)

            @pl.loop(0, j + 1)
            def _(kc):
                e = jnp.exp2((sc[kc] - m) * scale)
                sc[kc] = e
                a = e[:, :128]
                for n in range(1, BT // 128):
                    a = a + e[:, n * 128:(n + 1) * 128]
                mx[...] += a

            r = 1.0 / jnp.sum(mx[...], axis=1, keepdims=True)

            def pv(kc):
                kr = pl.ds(pl.multiple_of(kc * BT, BT), BT)
                return dot((sc[kc] * r).astype(BF16), qkv[kr, v0:v0 + dh])

            acc[...] = pv(0)

            @pl.loop(1, j + 1)
            def _(kc):
                acc[...] += pv(kc)

            h[:, ff + g * dh:ff + (g + 1) * dh] = acc[...].astype(BF16)

    @pl.loop(0, nb)
    def _(b):
        j = lax.rem(b, jb)
        rows = pl.ds(pl.multiple_of(j * BT, BT), BT)

        @pl.loop(0, nq)
        def _(i):
            slot = lax.rem(i, NSLOT)
            wait(w_q(i, slot))

            @pl.when(i == 0)
            def _():
                start(w_q(2, 2))

                @pl.when(b + 1 < nb)
                def _():
                    x_copy(b + 1).start()

            @pl.when(i > 0)
            def _():
                start(w_f(i - 1, lax.rem(i - 1, NSLOT)))

            qkv[rows, pl.ds(pl.multiple_of(i * NT, NT), NT)] = dot(ln[...], wbuf[slot]).astype(BF16)

            @pl.when((i == 0) & (b > 1))
            def _():
                t5(b - 2)

            @pl.when((i == 1) & (b > 1))
            def _():
                t6(b - 2)

            @pl.when((i == 2) & (b > 0))
            def _():
                t1()

        @pl.when(b > 0)
        def _():
            xt_copy(b - 1).start()
            t1_send()

        attention(j)

        @pl.loop(0, nf)
        def _(i):
            slot = lax.rem(i, NSLOT)
            wait(w_f(i, slot))

            @pl.when(i < 2)
            def _():
                start(w_f(i + 2, lax.rem(i + 2, NSLOT)))

            @pl.when(i >= 2)
            def _():
                start(w_o(1 - c, i - 2, lax.rem(i + 2, NSLOT)))

            for n in range(2):
                g = gelu(dot(ln[...], wbuf[slot, :, n * sub:(n + 1) * sub]))
                h[:, pl.ds(pl.multiple_of(i * NT + n * sub, sub), sub)] = g.astype(BF16)

            @pl.when((i == 0) & (b > 0))
            def _():
                t2(b - 1)

            @pl.when((i == 1) & (b > 0))
            def _():
                t3(b - 1)

            @pl.when((i == nf - 1) & (b > 0))
            def _():
                t4_partner(b - 1)

        @pl.when(b + 1 < nb)
        def _():
            x_copy(b + 1).wait()

        @pl.loop(0, nx)
        def _(k):
            i = k + nq + nf
            slot = lax.rem(i, NSLOT)
            wait(w_o(1 - c, k, slot))

            @pl.when(k < 2)
            def _():
                start(w_o(1 - c, k + 2, lax.rem(i + 2, NSLOT)))

            @pl.when(k >= 2)
            def _():
                start(w_o(c, k - 2, lax.rem(i + 2, NSLOT)))

            pt[k] = dot(h[...], wbuf[slot, :ff + hw, :]).astype(BF16)
            layer_norm(k * LR, LR)

            @pl.when(k > 0)
            def _():
                ptile(k - 1).start()

            @pl.when((k == 3) & (b > 0))
            def _():
                t4(b - 1)

        for k in range(nx):
            i = nq + nf + nx + k
            slot = i % NSLOT
            wait(w_o(c, k, slot))
            if k < 2:
                start(w_o(c, k + 2, (i + 2) % NSLOT))
            else:
                @pl.when(b + 1 < nb)
                def _():
                    start(w_q(k - 2, (i + 2) % NSLOT))
            if k == 0:
                own[...] = dot(h[...], wbuf[slot, :ff + hw, :])
                layer_norm((nx + k) * LR, LR)
                ptile(nx - 1).start()
                ptile(0).wait_recv()
                cs[0] = (own[...] + pr[0].astype(F32)).astype(BF16)
            else:
                ptile(k).wait_recv()
                s = dot(h[...], wbuf[slot, :ff + hw, :]) + pr[k].astype(F32)
                layer_norm((nx + k) * LR, LR)
                if k < nx - 1:
                    cs[k] = s.astype(BF16)
                else:
                    own[...] = s
            if k == 1:
                rs_opp_r.start()
                rs_opp_l.start()
            if k == 2:
                rs_dir_r.start()
            if k == 3:
                rs_dir_l.start()

    last = nb - 1
    xt_copy(last).start()
    t1()
    t5(last - 1)
    t1_send()
    t6(last - 1)
    t2(last)
    t3(last)
    t4_partner(last)
    t4(last)
    t5(last)
    t6(last)


def solution(mesh):
    tp = mesh.shape['tp']

    def local(x, gamma, beta, wqkv, wo, w1, w2):
        b, s, d = x.shape
        hl, dh, _ = wo.shape
        ff = w1.shape[1]
        nx = tp // 2
        ntok = b * s
        hb = BT // 2
        any_ = pl.BlockSpec(memory_space=pl.ANY)
        vm = pl.BlockSpec(memory_space=pltpu.VMEM)
        dma = pltpu.SemaphoreType.DMA
        flops = 2 * ntok * d * (wqkv.shape[1] + 2 * ff + hl * dh)
        out = pl.pallas_call(
            functools.partial(kernel, tp, s, hl, dh),
            out_shape=jax.ShapeDtypeStruct((ntok, d), BF16),
            in_specs=[any_, vm, vm, any_, any_, any_, any_],
            out_specs=any_,
            scratch_shapes=[
                pltpu.VMEM((NSLOT, d, NT), BF16),
                pltpu.VMEM((BT, d), BF16),
                pltpu.VMEM((BT, d), BF16),
                pltpu.VMEM((s, wqkv.shape[1]), BF16),
                pltpu.VMEM((s // BT, BT, BT), F32),
                pltpu.VMEM((BT, ff + hl * dh), BF16),
                pltpu.VMEM((nx, BT, NT), BF16),
                pltpu.VMEM((nx, BT, NT), BF16),
                pltpu.VMEM((nx - 1, BT, NT), BF16),
                pltpu.VMEM((BT, NT), F32),
                pltpu.VMEM((4, hb, NT), BF16),
                pltpu.VMEM((2, hb, NT), BF16),
                pltpu.VMEM((BT, NT), BF16),
                pltpu.VMEM((BT, NT), BF16),
                pltpu.VMEM((BT, 128), F32),
                pltpu.VMEM((BT, dh), F32),
                dma((NSLOT,)), dma((NSLOT,)), dma, dma, dma,
                dma((nx,)), dma((nx,)), dma((14,)), dma((14,)),
            ],
            compiler_params=pltpu.CompilerParams(collective_id=0, has_side_effects=True,
                                                 vmem_limit_bytes=67043328),
            cost_estimate=pl.CostEstimate(flops=flops, bytes_accessed=8 * 2 * (w1.size * 2 + wqkv.size + wo.size),
                                          transcendentals=0),
        )(x.reshape(ntok, d), gamma.reshape(1, d), beta.reshape(1, d), wqkv, wo.reshape(hl * dh, d), w1, w2)
        return out.reshape(b, s, d)

    return jax.shard_map(local, mesh=mesh,
                         in_specs=(P('dp', None, None), P(None), P(None), P(None, 'tp'),
                                   P('tp', None, None), P(None, 'tp'), P('tp', None)),
                         out_specs=P('dp', None, None), check_vma=False)
```

time: 948 us -> 375 us (0.40)
  matrix products: 384 us -> 0 us
  Pallas kernels: 0 us -> 352 us
  waiting for transfers between devices: 338 us -> 0 us
  other arithmetic: 122 us -> 0 us
  local copies, waits for them, and re-layouts: 81.4 us -> 22.9 us
  between operations: 13.9 us -> 0.01 us
    dot_general x8 -> x0, matrix products: 384 us -> none  [the longest x1 145 us: local(): jnp.dot(hmid, w2, preferred_element_type=jnp.float32)]
    pallas_call x0 -> x1, Pallas kernels: none -> 352 us  [local(): pl.pallas_call(functools.partial(kernel, tp, s, hl, dh), out_shape=jax.Sh...]
    psum x1 -> x0, waiting for transfers between devices: 338 us -> none  [local(): total = lax.psum(part_sum, 'tp')]
    reduce_sum x4 -> x0, other arithmetic: 57.6 us -> none  [the longest x2 33.5 us: attend(): p = jax.nn.softmax(sc, axis=-1).astype(jnp.bfloat16)]
    convert_element_type x2 -> x0, other arithmetic: 56.5 us -> none  [the longest x1 33.1 us: local(): (x.astype(jnp.float32) + total.astype(jnp.float32).reshape(b, s, d)).asty...]
    reshape x1 -> x0, local copies, waits for them, and re-layouts: 47.7 us -> none  [local(): qkv.reshape(b, s, gl, hpg + 2, dh)]
    unnamed x4 -> x1, local copies, waits for them, and re-layouts: 0.01 us -> 22.9 us
    while x13 -> x0, local copies, waits for them, and re-layouts: 13.4 us -> none  [the longest x1 13.4 us: local(): lax.map(functools.partial(attend, hpg=hpg), qkv.reshape(b, s, gl, hpg + 2...]
  transfers between devices with their start and end apart: 1 -> 0, of which waited for: 1 -> 0; matrix products, arithmetic and copies ran while one was open for 0% -> 0% of each run, Pallas kernels for 0% -> 0%
where the time goes in v1:
time: 375 us
  Pallas kernels  352 us (94%)
  local copies, waits for them, and re-layouts  22.9 us (6%)
    pallas_call x1, Pallas kernels, local(): pl.pallas_call(functools.partial(kernel, tp, s, hl, dh), out_shape=jax.Sh...  352 us
    unnamed x1, local copies, waits for them, and re-layouts  22.9 us

profile of v1, /device:TPU:81, one launch (start us, length us, event | category | flops | bytes accessed | tf_op | source)
XLA Modules:
  0.0 375.1 jit_solution(16642342711958103565)
XLA Ops:
  0.0 352.2 %shard_map.73 = bf16[4096,4096]{1,0:T(8,128)(2,1)} custom-call(bf16[4096,4096]{1,0:T(8,128)(2,1)} %bitcast.6, f32[1,4096]{1,0:T(1,128)} %bitcast.8, f32[1,4096]{1,0:T(1,128)} %bitcast.9, bf16[4096,1536]{1,0:T(8,128)(2,1)} %wqkv.1, bf16[512,4096]{1,0:T(8,128)(2,1)} %bitcast.7, bf16[4096,2048]{1,0:T(8,128)(2,1)} %w1.1, bf16[2048,4096]{1,0:T(8,128)(2,1)} %w2.1), custom_call_target="tpu_custom_call" | custom-call | flops 206158430208 | bytes 402653184 | tf_op jit(solution)/shard_map/pallas_call | solution.py:437
  352.2 22.9 %copy.9 = bf16[2,2048,4096]{2,1,0:T(8,128)(2,1)} copy(bf16[2,2048,4096]{2,1,0:T(8,128)(2,1)} %bitcast.5) | data formatting | bytes 67108864

commit v2 on v0

v2 whole, which is shorter than its diff:
```python
import functools

import jax
import jax.numpy as jnp
from jax import lax
from jax.experimental import pallas as pl
from jax.experimental.pallas import tpu as pltpu
from jax.sharding import PartitionSpec as P

MESH = pl.DeviceIdType.MESH
F32 = jnp.float32
BF16 = jnp.bfloat16
BT = 512
NT = 512
NSLOT = 4
NKIND = 14
T2STEP = 3
LOG2E = 1.4426950408889634


def dot(a, b):
    return jnp.dot(a, b, preferred_element_type=F32)


def gelu(x):
    return 0.5 * x * (1.0 + lax.erf(x * 0.7071067811865476))


def kernel(tp, seq, heads, dh,
           x, gamma, beta, wqkv, wo, w1, w2, y,
           wbuf, xbuf, ln, qkv, sc, h, pt, pr, cs, own, rs, relay, yt, xt, mx, ls, acc,
           wsem, wosem, xsem, xtsem, ysem, psend, precv, ssem, rsem):
    t = lax.axis_index('tp')
    nx = tp // 2
    d, c = t // 2, t % 2
    left = lax.rem(d + nx - 1, nx)
    right = lax.rem(d + 1, nx)
    opp = lax.rem(d + 2, nx)
    partner = {'tp': d * 2 + (1 - c)}
    dev_l = {'tp': left * 2 + c}
    dev_r = {'tp': right * 2 + c}

    ntok, dm = x.shape
    nb = ntok // BT
    jb = seq // BT
    hw = heads * dh
    ff = w1.shape[1]
    nq = wqkv.shape[1] // NT
    nf = ff // NT
    hb = BT // 2
    LR = BT // (2 * nx)
    sub = NT // 2

    def tile(cc, o):
        return pl.multiple_of((cc * nx + o) * NT, NT)

    def ds_rows(b, off=0, n=BT):
        return pl.ds(pl.multiple_of(b * BT + off, hb), n)

    def w_q(i, slot):
        return [pltpu.make_async_copy(wqkv.at[:, pl.ds(pl.multiple_of(i * NT, NT), NT)], wbuf.at[slot], wsem.at[slot])]

    def w_f(i, slot):
        return [pltpu.make_async_copy(w1.at[:, pl.ds(pl.multiple_of(i * NT, NT), NT)], wbuf.at[slot], wsem.at[slot])]

    owners = (opp, right, left, d)

    def w_o(cc, k, slot):
        col = tile(cc, owners[k])
        return [pltpu.make_async_copy(w2.at[:, pl.ds(col, NT)], wbuf.at[slot, pl.ds(0, ff)], wsem.at[slot]),
                pltpu.make_async_copy(wo.at[:, pl.ds(col, NT)], wbuf.at[slot, pl.ds(ff, hw)], wosem.at[slot])]

    def loads(step):
        o = 2 * (step % 2)
        if step == 0:
            return w_q(0, o) + w_q(1, o + 1)
        if step == 1:
            return w_q(2, o)
        if step < 4:
            n = 2 * (step - 2)
            return w_f(n, o) + w_f(n + 1, o + 1)
        n = 2 * (step % 2)
        cc = 1 - c if step < 6 else c
        return w_o(cc, n, o) + w_o(cc, n + 1, o + 1)

    def start(copies):
        for cp in copies:
            cp.start()

    def wait(copies):
        for cp in copies:
            cp.wait()

    def par(b):
        return b % 2 if isinstance(b, int) else lax.rem(b, 2)

    def rc(i, b, src, dst, dev):
        n = i + NKIND * par(b)
        return pltpu.make_async_remote_copy(src_ref=src, dst_ref=dst, send_sem=ssem.at[n], recv_sem=rsem.at[n],
                                            device_id=dev, device_id_type=MESH)

    rows_a, rows_b = pl.ds(0, hb), pl.ds(hb, hb)

    def rs_opp(b):
        return rc(0, b, cs.at[0, rows_b], relay.at[0], dev_r), rc(1, b, cs.at[0, rows_a], relay.at[1], dev_l)

    def rs_dir_r(b):
        return rc(2, b, cs.at[1, rows_a], rs.at[4 * par(b)], dev_r)

    def rs_dir_l(b):
        return rc(3, b, cs.at[2, rows_b], rs.at[4 * par(b) + 1], dev_l)

    def rs_cmb(b):
        return (rc(4, b, cs.at[1, rows_b], rs.at[4 * par(b) + 2], dev_r),
                rc(5, b, cs.at[2, rows_a], rs.at[4 * par(b) + 3], dev_l))

    def y_tile(b, cc, o, off, n):
        return y.at[ds_rows(b, off, n), pl.ds(tile(cc, o), NT)]

    def ag_own(b):
        dst = y_tile(b, c, d, 0, BT)
        return [rc(6, b, yt, dst, dev_r), rc(7, b, yt, dst, dev_l), rc(8, b, yt, dst, partner)]

    def ag_own_l(b):
        return rc(6, b, yt, y_tile(b, c, left, 0, BT), dev_r)

    def ag_own_r(b):
        return rc(7, b, yt, y_tile(b, c, right, 0, BT), dev_l)

    def ag_own_p(b):
        return rc(8, b, yt, y_tile(b, 1 - c, d, 0, BT), partner)

    def fwd_b(b, o):
        ref = y_tile(b, c, o, hb, hb)
        return rc(9, b, ref, ref, dev_r)

    def fwd_a(b, o):
        ref = y_tile(b, c, o, 0, hb)
        return rc(10, b, ref, ref, dev_l)

    def to_partner(i, b, cc, o):
        ref = y_tile(b, cc, o, 0, BT)
        return rc(i, b, ref, ref, partner)

    def ag_fwd(b):
        return [fwd_b(b, left), fwd_a(b, right), to_partner(11, b, c, left), to_partner(12, b, c, right)]

    def ptile(k):
        return pltpu.make_async_remote_copy(src_ref=pt.at[k], dst_ref=pr.at[k], send_sem=psend.at[k],
                                            recv_sem=precv.at[k], device_id=partner, device_id_type=MESH)

    def xt_copy(b):
        return pltpu.make_async_copy(x.at[ds_rows(b), pl.ds(tile(c, d), NT)], xt, xtsem)

    def yt_copy(b):
        return pltpu.make_async_copy(yt, y.at[ds_rows(b), pl.ds(tile(c, d), NT)], ysem)

    def x_copy(b):
        return pltpu.make_async_copy(x.at[ds_rows(b)], xbuf, xsem)

    def layer_norm(r0, n):
        for i in range(n // 16):
            r = pl.ds(pl.multiple_of(r0 + i * 16, 16), 16)
            v = xbuf[r, :].astype(F32)
            mu = jnp.sum(v, axis=-1, keepdims=True) * (1.0 / dm)
            v = v - mu
            var = jnp.sum(v * v, axis=-1, keepdims=True) * (1.0 / dm)
            ln[r, :] = (v * lax.rsqrt(var + 1e-5) * gamma[...] + beta[...]).astype(BF16)

    def t1(b):
        for cp in rs_opp(b):
            cp.wait_recv()
        cs[1, hb:, :] = (cs[1, hb:, :].astype(F32) + relay[0].astype(F32)).astype(BF16)
        cs[2, :hb, :] = (cs[2, :hb, :].astype(F32) + relay[1].astype(F32)).astype(BF16)
        for k in range(nx):
            ptile(k).wait_send()

    def t1_send(b):
        start(rs_cmb(b))

    def t2(b):
        rs_dir_r(b).wait_recv()
        rs_dir_l(b).wait_recv()
        for cp in rs_cmb(b):
            cp.wait_recv()
        xt_copy(b).wait()
        n = 4 * par(b)

        def rows(r, p, q):
            tot = own[r, :] + (rs[n + p].astype(F32) + rs[n + q].astype(F32))
            yt[r, :] = (xt[r, :].astype(F32) + tot.astype(BF16).astype(F32)).astype(BF16)
        rows(slice(0, hb), 0, 3)
        rows(slice(hb, BT), 1, 2)

    def t3(b):
        start(ag_own(b))
        yt_copy(b).start()

    def rs_sent(b):
        for cp in (*rs_opp(b), rs_dir_r(b), rs_dir_l(b), *rs_cmb(b)):
            cp.wait_send()

    def t4_wait(b):
        ag_own_l(b).wait_recv()
        ag_own_r(b).wait_recv()

    def t4_send(b):
        start(ag_fwd(b))
        for cp in ag_own(b):
            cp.wait_send()
        yt_copy(b).wait()

    def t5(b):
        fwd_b(b, opp).wait_recv()
        fwd_a(b, opp).wait_recv()
        to_partner(13, b, c, opp).start()

    def t6(b):
        to_partner(11, b, 1 - c, left).wait_recv()
        to_partner(12, b, 1 - c, right).wait_recv()
        to_partner(13, b, 1 - c, opp).wait_recv()
        for cp in ag_fwd(b):
            cp.wait_send()
        to_partner(13, b, c, opp).wait_send()

    x_copy(0).start()
    start(loads(0))
    bar = pltpu.get_barrier_semaphore()
    for dev in (dev_l, dev_r, partner):
        pl.semaphore_signal(bar, inc=1, device_id=dev, device_id_type=MESH)
    x_copy(0).wait()

    @pl.loop(0, 2 * nx)
    def _(i):
        layer_norm(i * LR, LR)

    pl.semaphore_wait(bar, 3)

    nl = BT // 128

    def scores(j):
        qr = pl.ds(pl.multiple_of(j * BT, BT), BT)
        q0 = [g * 3 * dh for g in range(heads)]

        def lanes(s):
            m = s[:, :128]
            for n in range(1, nl):
                m = jnp.maximum(m, s[:, n * 128:(n + 1) * 128])
            return m

        def qk(g, kc):
            kr = pl.ds(pl.multiple_of(kc * BT, BT), BT)
            return lax.dot_general(qkv[qr, q0[g]:q0[g] + dh], qkv[kr, q0[g] + dh:q0[g] + 2 * dh],
                                   (((1,), (1,)), ((), ())), preferred_element_type=F32)

        keep = lax.broadcasted_iota(jnp.int32, (BT, BT), 0) >= lax.broadcasted_iota(jnp.int32, (BT, BT), 1)
        for g in range(heads):
            s = jnp.where(keep, qk(g, j), -1e30)
            sc[g, j] = s
            mx[g] = lanes(s)

        @pl.loop(0, j)
        def _(kc):
            for g in range(heads):
                s = qk(g, kc)
                sc[g, kc] = s
                mx[g] = jnp.maximum(mx[g], lanes(s))

        for g in range(heads):
            mx[g] = jnp.broadcast_to(jnp.max(mx[g], axis=1, keepdims=True), (BT, 128))
            ls[g] = jnp.zeros((BT, 128), F32)

    def exponentials(j):
        scale = (dh ** -0.5) * LOG2E

        @pl.loop(0, j + 1)
        def _(kc):
            for g in range(heads):
                m = mx[g]
                a = ls[g]
                for n in range(nl):
                    r = slice(n * 128, (n + 1) * 128)
                    e = jnp.exp2((sc[g, kc, :, r] - m) * scale)
                    sc[g, kc, :, r] = e
                    a = a + e
                ls[g] = a

    def values(j):
        for g in range(heads):
            r = 1.0 / jnp.sum(ls[g], axis=1, keepdims=True)
            ls[g] = jnp.broadcast_to(r, (BT, 128))

        def pv(g, kc):
            kr = pl.ds(pl.multiple_of(kc * BT, BT), BT)
            r = ls[g]
            p = jnp.concatenate([(sc[g, kc, :, n * 128:(n + 1) * 128] * r).astype(BF16) for n in range(nl)], axis=1)
            return dot(p, qkv[kr, g * 3 * dh + 2 * dh:(g + 1) * 3 * dh])

        for g in range(heads):
            acc[g] = pv(g, 0)

        @pl.loop(1, j + 1)
        def _(kc):
            for g in range(heads):
                acc[g] += pv(g, kc)

        for g in range(heads):
            h[:, ff + g * dh:ff + (g + 1) * dh] = acc[g].astype(BF16)

    @pl.loop(0, nb)
    def _(b):
        j = lax.rem(b, jb)
        rows = pl.ds(pl.multiple_of(j * BT, BT), BT)

        def begin(step):
            wait(loads(step))
            if step < 7:
                start(loads(step + 1))
            else:
                @pl.when(b + 1 < nb)
                def _():
                    start(loads(0))

        def w(step, n, depth=dm):
            return wbuf[2 * (step % 2) + n, :depth, :]

        begin(0)

        @pl.when(b > 0)
        def _():
            rs_dir_l(b - 1).start()
            xt_copy(b - 1).start()

        @pl.when(b + 1 < nb)
        def _():
            x_copy(b + 1).start()

        for n in range(2):
            qkv[rows, n * NT:(n + 1) * NT] = dot(ln[...], w(0, n)).astype(BF16)
        begin(1)
        qkv[rows, 2 * NT:3 * NT] = dot(ln[...], w(1, 0)).astype(BF16)

        @pl.when(b > 1)
        def _():
            t4_wait(b - 2)

        @pl.when(b > 0)
        def _():
            t1(b - 1)

        scores(j)

        @pl.when(b > 0)
        def _():
            t1_send(b - 1)

        @pl.when(b > 1)
        def _():
            t4_send(b - 2)

        exponentials(j)
        values(j)

        for step in (2, 3):
            begin(step)
            for n in range(2):
                i = 2 * (step - 2) + n
                h[:, i * NT:(i + 1) * NT] = gelu(dot(ln[...], w(step, n))).astype(BF16)
            if step == T2STEP:
                @pl.when(b > 0)
                def _():
                    t2(b - 1)

        @pl.when(b + 1 < nb)
        def _():
            x_copy(b + 1).wait()

        for step in (4, 5):
            begin(step)
            if step == 4:
                @pl.when(b > 0)
                def _():
                    t3(b - 1)
            else:
                @pl.when(b > 0)
                def _():
                    ag_own_p(b - 1).wait_recv()
                    rs_sent(b - 1)

                ptile(0).start()
                ptile(1).start()
            for n in range(2):
                pt[2 * (step - 4) + n] = dot(h[...], w(step, n, ff + hw)).astype(BF16)
                layer_norm((2 * (step - 4) + n) * LR, LR)

        @pl.when(b > 1)
        def _():
            t5(b - 2)

        begin(6)
        ptile(2).start()
        ptile(3).start()
        ptile(0).wait_recv()
        ptile(1).wait_recv()
        for n in range(2):
            cs[n] = (dot(h[...], w(6, n, ff + hw)) + pr[n].astype(F32)).astype(BF16)
            layer_norm((4 + n) * LR, LR)
        begin(7)
        start(rs_opp(b))
        rs_dir_r(b).start()
        ptile(2).wait_recv()
        ptile(3).wait_recv()
        cs[2] = (dot(h[...], w(7, 0, ff + hw)) + pr[2].astype(F32)).astype(BF16)
        layer_norm(6 * LR, LR)
        own[...] = dot(h[...], w(7, 1, ff + hw)) + pr[3].astype(F32)
        layer_norm(7 * LR, LR)

        @pl.when(b > 1)
        def _():
            t6(b - 2)

    last = nb - 1
    rs_dir_l(last).start()
    xt_copy(last).start()
    t4_wait(last - 1)
    t1(last)
    t1_send(last)
    t4_send(last - 1)
    t2(last)
    t3(last)
    t5(last - 1)
    ag_own_p(last).wait_recv()
    rs_sent(last)
    t6(last - 1)
    t4_wait(last)
    t4_send(last)
    t5(last)
    t6(last)


def solution(mesh):
    tp = mesh.shape['tp']

    def local(x, gamma, beta, wqkv, wo, w1, w2):
        b, s, d = x.shape
        hl, dh, _ = wo.shape
        ff = w1.shape[1]
        nx = tp // 2
        ntok = b * s
        hb = BT // 2
        any_ = pl.BlockSpec(memory_space=pl.ANY)
        vm = pl.BlockSpec(memory_space=pltpu.VMEM)
        dma = pltpu.SemaphoreType.DMA
        flops = 2 * ntok * d * (wqkv.shape[1] + 2 * ff + hl * dh)
        out = pl.pallas_call(
            functools.partial(kernel, tp, s, hl, dh),
            out_shape=jax.ShapeDtypeStruct((ntok, d), BF16),
            in_specs=[any_, vm, vm, any_, any_, any_, any_],
            out_specs=any_,
            scratch_shapes=[
                pltpu.VMEM((NSLOT, d, NT), BF16),
                pltpu.VMEM((BT, d), BF16),
                pltpu.VMEM((BT, d), BF16),
                pltpu.VMEM((s, wqkv.shape[1]), BF16),
                pltpu.VMEM((hl, s // BT, BT, BT), F32),
                pltpu.VMEM((BT, ff + hl * dh), BF16),
                pltpu.VMEM((nx, BT, NT), BF16),
                pltpu.VMEM((nx, BT, NT), BF16),
                pltpu.VMEM((nx - 1, BT, NT), BF16),
                pltpu.VMEM((BT, NT), F32),
                pltpu.VMEM((8, hb, NT), BF16),
                pltpu.VMEM((2, hb, NT), BF16),
                pltpu.VMEM((BT, NT), BF16),
                pltpu.VMEM((BT, NT), BF16),
                pltpu.VMEM((hl, BT, 128), F32),
                pltpu.VMEM((hl, BT, 128), F32),
                pltpu.VMEM((hl, BT, dh), F32),
                dma((NSLOT,)), dma((NSLOT,)), dma, dma, dma,
                dma((nx,)), dma((nx,)), dma((2 * NKIND,)), dma((2 * NKIND,)),
            ],
            compiler_params=pltpu.CompilerParams(collective_id=0, has_side_effects=True,
                                                 vmem_limit_bytes=67043328),
            cost_estimate=pl.CostEstimate(flops=flops, bytes_accessed=8 * 2 * (w1.size * 2 + wqkv.size + wo.size),
                                          transcendentals=0),
        )(x.reshape(ntok, d), gamma.reshape(1, d), beta.reshape(1, d), wqkv, wo.reshape(hl * dh, d), w1, w2)
        return out.reshape(b, s, d)

    return jax.shard_map(local, mesh=mesh,
                         in_specs=(P('dp', None, None), P(None), P(None), P(None, 'tp'),
                                   P('tp', None, None), P(None, 'tp'), P('tp', None)),
                         out_specs=P('dp', None, None), check_vma=False)
```

time: 948 us -> 350 us (0.37)
  matrix products: 384 us -> 0 us
  waiting for transfers between devices: 338 us -> 0 us
  Pallas kernels: 0 us -> 327 us
  other arithmetic: 122 us -> 0 us
  local copies, waits for them, and re-layouts: 81.4 us -> 22.9 us
  between operations: 13.9 us -> 0.01 us
    dot_general x8 -> x0, matrix products: 384 us -> none  [the longest x1 145 us: local(): jnp.dot(hmid, w2, preferred_element_type=jnp.float32)]
    psum x1 -> x0, waiting for transfers between devices: 338 us -> none  [local(): total = lax.psum(part_sum, 'tp')]
    pallas_call x0 -> x1, Pallas kernels: none -> 327 us  [local(): pl.pallas_call(functools.partial(kernel, tp, s, hl, dh), out_shape=jax.Sh...]
    reduce_sum x4 -> x0, other arithmetic: 57.6 us -> none  [the longest x2 33.5 us: attend(): p = jax.nn.softmax(sc, axis=-1).astype(jnp.bfloat16)]
    convert_element_type x2 -> x0, other arithmetic: 56.5 us -> none  [the longest x1 33.1 us: local(): (x.astype(jnp.float32) + total.astype(jnp.float32).reshape(b, s, d)).asty...]
    reshape x1 -> x0, local copies, waits for them, and re-layouts: 47.7 us -> none  [local(): qkv.reshape(b, s, gl, hpg + 2, dh)]
    unnamed x4 -> x1, local copies, waits for them, and re-layouts: 0.01 us -> 22.9 us
    while x13 -> x0, local copies, waits for them, and re-layouts: 13.4 us -> none  [the longest x1 13.4 us: local(): lax.map(functools.partial(attend, hpg=hpg), qkv.reshape(b, s, gl, hpg + 2...]
  transfers between devices with their start and end apart: 1 -> 0, of which waited for: 1 -> 0; matrix products, arithmetic and copies ran while one was open for 0% -> 0% of each run, Pallas kernels for 0% -> 0%
where the time goes in v2:
time: 350 us
  Pallas kernels  327 us (93%)
  local copies, waits for them, and re-layouts  22.9 us (7%)
    pallas_call x1, Pallas kernels, local(): pl.pallas_call(functools.partial(kernel, tp, s, hl, dh), out_shape=jax.Sh...  327 us
    unnamed x1, local copies, waits for them, and re-layouts  22.9 us

profile of v2, /device:TPU:81, one launch (start us, length us, event | category | flops | bytes accessed | tf_op | source)
XLA Modules:
  0.0 350.1 jit_solution(9483381958441421380)
XLA Ops:
  0.0 327.2 %shard_map.73 = bf16[4096,4096]{1,0:T(8,128)(2,1)} custom-call(bf16[4096,4096]{1,0:T(8,128)(2,1)} %bitcast.6, f32[1,4096]{1,0:T(1,128)} %bitcast.8, f32[1,4096]{1,0:T(1,128)} %bitcast.9, bf16[4096,1536]{1,0:T(8,128)(2,1)} %wqkv.1, bf16[512,4096]{1,0:T(8,128)(2,1)} %bitcast.7, bf16[4096,2048]{1,0:T(8,128)(2,1)} %w1.1, bf16[2048,4096]{1,0:T(8,128)(2,1)} %w2.1), custom_call_target="tpu_custom_call" | custom-call | flops 206158430208 | bytes 402653184 | tf_op jit(solution)/shard_map/pallas_call | solution.py:455
  327.2 22.9 %copy.9 = bf16[2,2048,4096]{2,1,0:T(8,128)(2,1)} copy(bf16[2,2048,4096]{2,1,0:T(8,128)(2,1)} %bitcast.5) | data formatting | bytes 67108864

commit v3 on v2

--- a/solution.py
+++ b/solution.py
@@ -28,7 +28,7 @@
 
 def kernel(tp, seq, heads, dh,
            x, gamma, beta, wqkv, wo, w1, w2, y,
-           wbuf, xbuf, ln, qkv, sc, h, pt, pr, cs, own, rs, relay, yt, xt, mx, ls, acc,
+           wbuf, xbuf, ln, qkv, sc, h, pt, pr, cs, own, rs, relay, yt, xt, mx, ls,
            wsem, wosem, xsem, xtsem, ysem, psend, precv, ssem, rsem):
     t = lax.axis_index('tp')
     nx = tp // 2
@@ -239,7 +239,7 @@
     nl = BT // 128
 
     def scores(j):
-        qr = pl.ds(pl.multiple_of(j * BT, BT), BT)
+        qr = slice(j * BT, (j + 1) * BT)
         q0 = [g * 3 * dh for g in range(heads)]
 
         def lanes(s):
@@ -249,63 +249,43 @@
             return m
 
         def qk(g, kc):
-            kr = pl.ds(pl.multiple_of(kc * BT, BT), BT)
+            kr = slice(kc * BT, (kc + 1) * BT)
             return lax.dot_general(qkv[qr, q0[g]:q0[g] + dh], qkv[kr, q0[g] + dh:q0[g] + 2 * dh],
                                    (((1,), (1,)), ((), ())), preferred_element_type=F32)
 
         keep = lax.broadcasted_iota(jnp.int32, (BT, BT), 0) >= lax.broadcasted_iota(jnp.int32, (BT, BT), 1)
         for g in range(heads):
-            s = jnp.where(keep, qk(g, j), -1e30)
-            sc[g, j] = s
-            mx[g] = lanes(s)
-
-        @pl.loop(0, j)
-        def _(kc):
-            for g in range(heads):
+            m = None
+            for kc in range(j + 1):
                 s = qk(g, kc)
+                if kc == j:
+                    s = jnp.where(keep, s, -1e30)
                 sc[g, kc] = s
-                mx[g] = jnp.maximum(mx[g], lanes(s))
-
+                m = lanes(s) if m is None else jnp.maximum(m, lanes(s))
+            mx[g] = jnp.broadcast_to(jnp.max(m, axis=1, keepdims=True), (BT, 128))
+
+    def values(j):
+        scale = (dh ** -0.5) * LOG2E
         for g in range(heads):
-            mx[g] = jnp.broadcast_to(jnp.max(mx[g], axis=1, keepdims=True), (BT, 128))
-            ls[g] = jnp.zeros((BT, 128), F32)
-
-    def exponentials(j):
-        scale = (dh ** -0.5) * LOG2E
-
-        @pl.loop(0, j + 1)
-        def _(kc):
-            for g in range(heads):
-                m = mx[g]
-                a = ls[g]
+            m = mx[g]
+            a = None
+            for kc in range(j + 1):
                 for n in range(nl):
                     r = slice(n * 128, (n + 1) * 128)
                     e = jnp.exp2((sc[g, kc, :, r] - m) * scale)
                     sc[g, kc, :, r] = e
-                    a = a + e
-                ls[g] = a
-
-    def values(j):
+                    a = e if a is None else a + e
+            ls[g] = jnp.broadcast_to(1.0 / jnp.sum(a, axis=1, keepdims=True), (BT, 128))
         for g in range(heads):
-            r = 1.0 / jnp.sum(ls[g], axis=1, keepdims=True)
-            ls[g] = jnp.broadcast_to(r, (BT, 128))
-
-        def pv(g, kc):
-            kr = pl.ds(pl.multiple_of(kc * BT, BT), BT)
             r = ls[g]
-            p = jnp.concatenate([(sc[g, kc, :, n * 128:(n + 1) * 128] * r).astype(BF16) for n in range(nl)], axis=1)
-            return dot(p, qkv[kr, g * 3 * dh + 2 * dh:(g + 1) * 3 * dh])
-
-        for g in range(heads):
-            acc[g] = pv(g, 0)
-
-        @pl.loop(1, j + 1)
-        def _(kc):
-            for g in range(heads):
-                acc[g] += pv(g, kc)
-
-        for g in range(heads):
-            h[:, ff + g * dh:ff + (g + 1) * dh] = acc[g].astype(BF16)
+            p = jnp.concatenate([(sc[g, kc, :, n * 128:(n + 1) * 128] * r).astype(BF16)
+                                 for kc in range(j + 1) for n in range(nl)], axis=1)
+            v0 = g * 3 * dh + 2 * dh
+            h[:, ff + g * dh:ff + (g + 1) * dh] = dot(p, qkv[:(j + 1) * BT, v0:v0 + dh]).astype(BF16)
+
+    def for_block(j, f):
+        for n in range(jb):
+            pl.when(j == n)(functools.partial(f, n))
 
     @pl.loop(0, nb)
     def _(b):
@@ -348,7 +328,7 @@
         def _():
             t1(b - 1)
 
-        scores(j)
+        for_block(j, scores)
 
         @pl.when(b > 0)
         def _():
@@ -358,8 +338,7 @@
         def _():
             t4_send(b - 2)
 
-        exponentials(j)
-        values(j)
+        for_block(j, values)
 
         for step in (2, 3):
             begin(step)
@@ -474,7 +453,6 @@
                 pltpu.VMEM((BT, NT), BF16),
                 pltpu.VMEM((hl, BT, 128), F32),
                 pltpu.VMEM((hl, BT, 128), F32),
-                pltpu.VMEM((hl, BT, dh), F32),
                 dma((NSLOT,)), dma((NSLOT,)), dma, dma, dma,
                 dma((nx,)), dma((nx,)), dma((2 * NKIND,)), dma((2 * NKIND,)),
             ],

time: 350 us -> 342 us (0.977)
  Pallas kernels: 327 us -> 319 us
    pallas_call x1, Pallas kernels: 327 us -> 319 us  [local(): pl.pallas_call(functools.partial(kernel, tp, s, hl, dh), out_shape=jax.Sh...]
where the time goes in v3:
time: 342 us
  Pallas kernels  319 us (93%)
  local copies, waits for them, and re-layouts  22.9 us (7%)
    pallas_call x1, Pallas kernels, local(): pl.pallas_call(functools.partial(kernel, tp, s, hl, dh), out_shape=jax.Sh...  319 us
    unnamed x1, local copies, waits for them, and re-layouts  22.9 us

profile of v3, /device:TPU:81, one launch (start us, length us, event | category | flops | bytes accessed | tf_op | source)
XLA Modules:
  0.0 341.7 jit_solution(3220520138079441180)
XLA Ops:
  0.0 318.7 %shard_map.73 = bf16[4096,4096]{1,0:T(8,128)(2,1)} custom-call(bf16[4096,4096]{1,0:T(8,128)(2,1)} %bitcast.6, f32[1,4096]{1,0:T(1,128)} %bitcast.8, f32[1,4096]{1,0:T(1,128)} %bitcast.9, bf16[4096,1536]{1,0:T(8,128)(2,1)} %wqkv.1, bf16[512,4096]{1,0:T(8,128)(2,1)} %bitcast.7, bf16[4096,2048]{1,0:T(8,128)(2,1)} %w1.1, bf16[2048,4096]{1,0:T(8,128)(2,1)} %w2.1), custom_call_target="tpu_custom_call" | custom-call | flops 206158430208 | bytes 402653184 | tf_op jit(solution)/shard_map/pallas_call | solution.py:434
  318.8 22.9 %copy.9 = bf16[2,2048,4096]{2,1,0:T(8,128)(2,1)} copy(bf16[2,2048,4096]{2,1,0:T(8,128)(2,1)} %bitcast.5) | data formatting | bytes 67108864
